TPU v7x, 32 devices: a whole 2x2x4 slice. The times are simulated.
32 devices in a mesh: grp: 2 (over y), dev: 16 (over z, x, core).
Axes of the slice: x: 2, y: 2, z: 4, core: 2. Of those that a mesh axis runs over, the one named last changes fastest.
Arguments:
- pooled_grad: bfloat16 [4096, 32, 128], P(('grp', 'dev')), may hold values from -6 to 6
- row_ids: int32 [4096, 4, 32], P(('grp', 'dev')), may hold values from 0 to 1023
- scale_exps: int32 [4096, 32], P(('grp', 'dev')), may hold values from 0 to 3
- table_owner: int32 [32], replicated, may hold values from 0 to 31, each once
- dense_acts: bfloat16 [4096, 512], P(('grp', 'dev')), may hold values from -6 to 6
- dense_cot: bfloat16 [4096, 512], P(('grp', 'dev')), may hold values from -0.1875 to 0.1875
Outputs:
- table_grad: float32 [32, 1024, 128], P('dev')
- weight_grad: float32 [512, 512], replicated
- bias_grad: float32 [512], replicated
Inputs may be any that keep to these rules, and one draw needn't show every extreme that they name: Table t's rows are accumulated into slot table_owner[t]; each slot belongs to exactly one table.
All inputs are finite; a program needn't handle non-finite values.
Results may differ from a plain program's by a relative error of at most 0.0003.
Values may be sent and summed in bfloat16 or wider, within the bound.
A program may use at most 128 MiB of HBM per device.

v0:
```python
import math
import jax
import jax.numpy as jnp
from jax import lax
from jax.sharding import PartitionSpec as P

ROWS = 1024


def powers(exps):
    return (
        1.0
        + (exps >= 1).astype(jnp.float32)
        + 2.0 * (exps >= 2).astype(jnp.float32)
        + 4.0 * (exps >= 3).astype(jnp.float32)
    )


def accumulate(grads, indices, exps):
    samples = grads.shape[0]
    slots = grads.shape[2]
    pool_len = indices.shape[3]
    block_rows = math.gcd(samples, 1024)
    row_axis = lax.broadcasted_iota(jnp.int32, (ROWS, 1), 0)
    results = []
    for slot_pos in range(slots):
        factor = powers(exps[:, 0, slot_pos])
        restored = (grads[:, 0, slot_pos, :].astype(jnp.float32) * factor[:, None]).astype(
            jnp.bfloat16
        )
        row_index = indices[:, 0, slot_pos, :]

        def add_block(count, running, restored=restored, row_index=row_index):
            offset = count * block_rows
            values = lax.dynamic_slice_in_dim(restored, offset, block_rows, 0)
            picked = lax.dynamic_slice_in_dim(row_index, offset, block_rows, 0)
            counts = jnp.zeros((ROWS, block_rows), jnp.float32)
            for lookup in range(pool_len):
                counts = counts + (picked[:, lookup][None, :] == row_axis).astype(jnp.float32)
            return running + jnp.dot(
                counts.astype(jnp.bfloat16), values, preferred_element_type=jnp.float32
            )

        start_grad = jnp.zeros((ROWS, grads.shape[3]), jnp.float32)
        results.append(lax.fori_loop(0, samples // block_rows, add_block, start_grad))
    return jnp.stack(results, 0)


def per_device(pooled_grad, row_ids, scale_exps, table_owner, dense_acts, dense_cot):
    batch_rows, tables, feat_width = pooled_grad.shape
    dev_count = lax.axis_size("dev")
    per_owner = tables // dev_count
    pool_len = row_ids.shape[1]
    factor = powers(scale_exps)
    quantized = jnp.clip(pooled_grad.astype(jnp.float32) / factor[:, :, None], -1.0, 1.0).astype(
        jnp.bfloat16
    )
    slot_table = (
        jnp.zeros((tables,), jnp.int32).at[table_owner].set(jnp.arange(tables, dtype=jnp.int32))
    )
    send_grads = jnp.take(quantized, slot_table, axis=1).reshape(
        batch_rows, dev_count, per_owner, feat_width
    )
    send_rows = jnp.transpose(
        jnp.take(row_ids, slot_table, axis=2).reshape(batch_rows, pool_len, dev_count, per_owner),
        (0, 2, 3, 1),
    )
    send_exps = jnp.take(scale_exps, slot_table, axis=1).reshape(batch_rows, dev_count, per_owner)
    weight_term = lax.dot_general(
        dense_acts, dense_cot, (((0,), (0,)), ((), ())), preferred_element_type=jnp.float32
    )
    bias_term = jnp.sum(dense_cot.astype(jnp.float32), axis=0)
    partial_grad = accumulate(
        lax.all_to_all(send_grads, "dev", split_axis=1, concat_axis=0, tiled=True),
        lax.all_to_all(send_rows, "dev", split_axis=1, concat_axis=0, tiled=True),
        lax.all_to_all(send_exps, "dev", split_axis=1, concat_axis=0, tiled=True),
    )
    table_grad = lax.psum(partial_grad, "grp")
    dense_parts = (
        lax.psum_scatter(weight_term, "dev", scatter_dimension=0, tiled=True),
        lax.psum_scatter(bias_term, "dev", scatter_dimension=0, tiled=True),
    )
    dense_parts = lax.psum((dense_parts[0], dense_parts[1]), "grp")
    weight_grad, bias_grad = (
        lax.all_gather(dense_parts[0], "dev", axis=0, tiled=True),
        lax.all_gather(dense_parts[1], "dev", axis=0, tiled=True),
    )
    return (table_grad, weight_grad, bias_grad)


def solution(mesh):
    return jax.shard_map(
        per_device,
        mesh=mesh,
        in_specs=(
            P(("grp", "dev"), None, None),
            P(("grp", "dev"), None, None),
            P(("grp", "dev"), None),
            P(),
            P(("grp", "dev"), None),
            P(("grp", "dev"), None),
        ),
        out_specs=(P("dev", None, None), P(), P()),
        check_vma=False,
    )
```

profile of v0, /device:TPU:0, one launch (start us, length us, event | category | flops | bytes accessed | tf_op | source)
XLA Modules:
  0.0 227.3 jit_solution(12590961035273388617)
XLA Ops:
  7.2 0.7 compare_select_fusion.5
  7.9 0.7 scatter_custom_fusion
  8.6 0.1 broadcast_in_dim.41
  8.7 1.3 gather_fusion.2
  10.0 0.7 broadcast_select_fusion.1
  10.7 7.4 %all-to-all-start.2 = ((s32[128,16,2]{0,2,1:T(2,128)}), s32[128,16,2]{0,2,1:T(2,128)S(1)}, u32[]{:S(2)}, u32[]{:S(2)}) async-start(s32[128,16,2]{0,2,1:T(2,128)} %broadcast_select_fusion.1), calls=%async_computation.2 | async-start | bytes 32768 | tf_op jit(solution)/shard_map/all_to_all | solution.py:76
  18.1 0.7 select_add_fusion
  18.8 0.6 gather_fusion
  19.5 0.6 copy-done.2
  20.1 1.4 clamp_convert_fusion
  21.5 0.7 fusion.14
  22.2 0.7 gather_fusion.1
  22.9 1.7 all-to-all-done.2
  24.6 4.4 %all-to-all-start = ((s32[128,16,2,4]{0,2,3,1:T(2,128)}), s32[128,16,2,4]{0,2,3,1:T(2,128)S(1)}, u32[]{:S(2)}, u32[]{:S(2)}) async-start(s32[128,16,2,4]{0,2,3,1:T(2,128)} %fusion.14), calls=%async_computation | async-start | bytes 131072 | tf_op jit(solution)/shard_map/all_to_all | solution.py:75
  29.0 1.1 broadcast_select_fusion
  30.1 5.8 %all-to-all-done = s32[128,16,2,4]{0,2,3,1:T(2,128)S(1)} async-done(((s32[128,16,2,4]{0,2,3,1:T(2,128)}), s32[128,16,2,4]{0,2,3,1:T(2,128)S(1)}, u32[]{:S(2)}, u32[]{:S(2)}) %all-to-all-start) | async-done | bytes 65568 | tf_op jit(solution)/shard_map/all_to_all | solution.py:75
  35.9 3.7 %all-to-all-start.1 = ((bf16[128,16,2,128]{3,0,2,1:T(8,128)(2,1)}), bf16[128,16,2,128]{3,0,2,1:T(8,128)(2,1)S(1)}, u32[]{:S(2)}, u32[]{:S(2)}) async-start(bf16[128,16,2,128]{3,0,2,1:T(8,128)(2,1)} %broadcast_select_fusion), calls=%async_computation.1 | async-start | bytes 2097152 | tf_op jit(solution)/shard_map/all_to_all | solution.py:74
  39.5 0.0 reduce-scatter.2.cloned.1.call-start
  39.6 1.3 fusion.25
  40.9 0.0 reduce-scatter.2.cloned.1.call-update
  40.9 0.0 all-reduce.5.cloned.1.call-start
  41.1 21.3 %all-to-all-done.1 = bf16[128,16,2,128]{3,0,2,1:T(8,128)(2,1)S(1)} async-done(((bf16[128,16,2,128]{3,0,2,1:T(8,128)(2,1)}), bf16[128,16,2,128]{3,0,2,1:T(8,128)(2,1)S(1)}, u32[]{:S(2)}, u32[]{:S(2)}) %all-to-all-start.1) | async-done | bytes 1048608 | tf_op jit(solution)/shard_map/all_to_all | solution.py:74
  62.4 0.1 copy.26
  62.5 0.7 fusion.13
  63.2 4.5 %while.31 = (s32[]{:T(128)}, f32[1024,128]{1,0:T(8,128)S(1)}, s32[2048,4]{0,1:T(4,128)S(1)}, bf16[2048,128]{1,0:T(8,128)(2,1)S(1)}, s32[]{:T(128)}, /*index=5*/s...) while((s32[]{:T(128)}, f32[1024,128]{1,0:T(8,128)S(1)}, ...), condition=%wide.region_4.5_spmd.clone.clone, body=%wide.region_3.4_spmd.clone.clone.sunk | while | flops 281280512 | bytes 1360101 | solution.py:45
  63.2 0.1 constant_dynamic-slice_fusion.5
  63.4 2.1 fusion.35
  65.5 0.1 constant_dynamic-slice_fusion.5
  65.6 2.1 fusion.35
  67.7 4.5 %while.30 = (s32[]{:T(128)}, f32[1024,128]{1,0:T(8,128)S(1)}, s32[2048,4]{0,1:T(4,128)S(1)}, bf16[2048,128]{1,0:T(8,128)(2,1)S(1)}, s32[]{:T(128)}, /*index=5*/s...) while((s32[]{:T(128)}, f32[1024,128]{1,0:T(8,128)S(1)}, ...), condition=%wide.region_2.3_spmd.clone.clone, body=%wide.region_1.2_spmd.clone.clone.sunk | while | flops 281280512 | bytes 1360101 | solution.py:45
  67.7 0.1 constant_dynamic-slice_fusion.4
  67.8 2.1 fusion.33
  69.9 0.1 constant_dynamic-slice_fusion.4
  70.1 2.1 fusion.33
  72.2 1.0 pad_maximum_fusion
  73.2 30.2 %reduce-scatter.2.cloned.1.call-done = f32[32,512]{1,0:T(8,128)} async-done(((f32[512,512]{1,0:T(8,128)}), f32[32,512]{1,0:T(8,128)}) %reduce-scatter.2.cloned.1.call-update) | async-done | bytes 65552 | tf_op jit(solution)/shard_map/reduce_scatter | solution.py:80
  103.5 0.0 all-reduce.5.cloned.1.call-update
  103.5 0.0 all-gather.2.cloned.1.call-start
  103.5 43.6 %all-reduce.5.cloned.1.call-done = (f32[2,1024,128]{2,1,0:T(8,128)}, f32[32,512]{1,0:T(8,128)}) async-done(((f32[2,1024,128]{2,1,0:T(8,128)}, f32[32,512]{1,0:T(8,128)}), (f32[2,1024,128]{2,1,0:T(8,128)}, f32[32,512]{1,0:T(8,128)})) %all-reduce.5.cloned.1.call-update) | async-done | bytes 1114128 | tf_op jit(solution)/shard_map/psum | solution.py:78
  147.1 0.0 all-gather.2.cloned.1.call-update
  147.1 0.6 fusion.24
  148.4 33.2 %all-reduce.1 = f32[512]{0:T(512)S(1)} all-reduce(f32[512]{0:T(512)S(1)} %convert_reduce_fusion), channel_id=3, replica_groups=mesh['grp'=2,'dev'=16] {'dev'}, use_global_device_ids=true, to_apply=%region_9.10.clone | all-reduce | flops 512 | bytes 4096
  181.6 0.1 dynamic-slice.2
  182.3 4.9 %psum.23 = f32[32]{0:T(128)S(1)} all-reduce(f32[32]{0:T(128)S(1)} %dynamic-slice.2), channel_id=1, replica_groups=mesh['grp'=2,'dev'=16] {'grp'}, use_global_device_ids=true, to_apply=%region_10.11 | all-reduce | flops 32 | bytes 256 | tf_op jit(solution)/shard_map/psum | solution.py:83
  187.3 0.2 dynamic-update-slice
  187.4 30.0 %all-reduce = f32[512]{0:T(512)} all-reduce(f32[512]{0:T(512)S(1)} %dynamic-update-slice), channel_id=1, replica_groups=mesh['grp'=2,'dev'=16] {'dev'}, use_global_device_ids=true, to_apply=%add | all-reduce | flops 512 | bytes 4096
  217.5 2.4 %copy.52 = f32[2,1024,128]{2,1,0:T(8,128)} copy(f32[2,1024,128]{2,1,0:T(8,128)} %get-tuple-element.448) | data formatting | bytes 2097152
  219.8 1.0 copy.53
  (25 shorter events, 0.2 us)
Async XLA Ops:
  7.2 32.4 %copy-start = (bf16[128,512]{1,0:T(8,128)(2,1)S(1)}, bf16[128,512]{1,0:T(8,128)(2,1)}, u32[]{:S(2)}) copy-start(bf16[128,512]{1,0:T(8,128)(2,1)} %param.14) | copy-start | bytes 393220
  7.2 11.7 %copy-start.1 = (s32[128,4,32]{0,2,1:T(8,128)S(1)}, s32[128,4,32]{0,2,1:T(8,128)}, u32[]{:S(2)}) copy-start(s32[128,4,32]{0,2,1:T(8,128)} %param.11) | copy-start | bytes 196612
  10.7 13.9 %all-to-all-start.2 = ((s32[128,16,2]{0,2,1:T(2,128)}), s32[128,16,2]{0,2,1:T(2,128)S(1)}, u32[]{:S(2)}, u32[]{:S(2)}) async-start(s32[128,16,2]{0,2,1:T(2,128)} %broadcast_select_fusion.1), calls=%async_computation.2 | async-start | bytes 32768 | tf_op jit(solution)/shard_map/all_to_all | solution.py:76
  18.8 1.2 copy-start.2
  24.6 11.3 %all-to-all-start = ((s32[128,16,2,4]{0,2,3,1:T(2,128)}), s32[128,16,2,4]{0,2,3,1:T(2,128)S(1)}, u32[]{:S(2)}, u32[]{:S(2)}) async-start(s32[128,16,2,4]{0,2,3,1:T(2,128)} %fusion.14), calls=%async_computation | async-start | bytes 131072 | tf_op jit(solution)/shard_map/all_to_all | solution.py:75
  30.1 9.5 %copy-start.4 = (bf16[128,512]{1,0:T(8,128)(2,1)S(1)}, bf16[128,512]{1,0:T(8,128)(2,1)}, u32[]{:S(2)}) copy-start(bf16[128,512]{1,0:T(8,128)(2,1)} %param.15) | copy-start | bytes 393220
  35.9 26.5 %all-to-all-start.1 = ((bf16[128,16,2,128]{3,0,2,1:T(8,128)(2,1)}), bf16[128,16,2,128]{3,0,2,1:T(8,128)(2,1)S(1)}, u32[]{:S(2)}, u32[]{:S(2)}) async-start(bf16[128,16,2,128]{3,0,2,1:T(8,128)(2,1)} %broadcast_select_fusion), calls=%async_computation.1 | async-start | bytes 2097152 | tf_op jit(solution)/shard_map/all_to_all | solution.py:74
  39.5 63.9 %reduce-scatter.2.cloned.1.call-start = ((), (), s32[]{:S(2)}) async-start(), calls=%async_computation.4 | async-start | bytes 1114112 | tf_op jit(solution)/shard_map/reduce_scatter | solution.py:80
  40.9 106.2 %all-reduce.5.cloned.1.call-start = ((), (), s32[]{:S(2)}) async-start(), calls=%async_computation.6 | async-start | bytes 2228224 | tf_op jit(solution)/shard_map/psum | solution.py:78
  73.2 73.9 %copy-start.5 = (u32[32]{0:T(128)S(1)}, u32[32]{0:T(128)}, u32[]{:S(2)}) copy-start(u32[32]{0:T(128)} %constant.132) | copy-start | bytes 388
  103.5 114.0 %all-gather.2.cloned.1.call-start = ((), (), s32[]{:S(2)}) async-start(), calls=%async_computation.5 | async-start | bytes 1114112 | tf_op jit(solution)/shard_map/all_gather | solution.py:85
  217.5 2.4 %copy-start.3 = (f32[512,512]{1,0:T(8,128)S(1)}, f32[512,512]{1,0:T(8,128)}, u32[]{:S(2)}) copy-start(f32[512,512]{1,0:T(8,128)} %all-gather.2.cloned.1.call-done) | copy-start | bytes 3145732
Sparse Core Ops, SparseCore 0:
  44.6 58.8 reduce-scatter.1
  106.4 40.6 all-reduce.4
  149.3 37.8 all-gather.1
where the time goes:
time: 228 us; the launch traced here: 227 us
  waiting for transfers between devices  103 us (45%)
  blocking collectives  68.2 us (30%)
  starting transfers between devices  15.5 us (7%)
  between operations  15.3 us (7%)
  matrix products  9.65 us (4%)
  local copies, waits for them, and re-layouts  8.8 us (4%)
  other arithmetic  7.24 us (3%)
    unnamed x2, blocking collectives  63.2 us
    psum x1, waiting for transfers between devices, per_device(): table_grad = lax.psum(partial_grad, 'grp')  43.6 us
    reduce_scatter x1, waiting for transfers between devices, per_device(): lax.psum_scatter(weight_term, 'dev', scatter_dimension=0, tiled=True)  30.2 us
    all_to_all x1, waiting for transfers between devices, per_device(): lax.all_to_all(send_grads, 'dev', split_axis=1, concat_axis=0, tiled=True)  21.3 us
    dot_general x4, matrix products, add_block(): jnp.dot(counts.astype(jnp.bfloat16), values, preferred_element_type=jnp.f...  8.36 us
    all_to_all x1, starting transfers between devices, per_device(): lax.all_to_all(send_exps, 'dev', split_axis=1, concat_axis=0, tiled=True)  7.39 us
    all_to_all x1, waiting for transfers between devices, per_device(): lax.all_to_all(send_rows, 'dev', split_axis=1, concat_axis=0, tiled=True)  5.76 us
    psum x1, blocking collectives, per_device(): dense_parts = lax.psum((dense_parts[0], dense_parts[1]), 'grp')  4.93 us
  transfers between devices with their start and end apart: 6, of which 5 were waited for; matrix products, arithmetic and copies ran while one was open for 8% of the time, Pallas kernels for 0%

commit v1 on v0

--- a/solution.py
+++ b/solution.py
@@ -75,7 +75,8 @@
         lax.all_to_all(send_rows, "dev", split_axis=1, concat_axis=0, tiled=True),
         lax.all_to_all(send_exps, "dev", split_axis=1, concat_axis=0, tiled=True),
     )
-    table_grad = lax.psum(partial_grad, "grp")
+    parts = lax.all_gather(partial_grad, "grp")
+    table_grad = jnp.sum(parts, axis=0)
     dense_parts = (
         lax.psum_scatter(weight_term, "dev", scatter_dimension=0, tiled=True),
         lax.psum_scatter(bias_term, "dev", scatter_dimension=0, tiled=True),

time: 228 us -> 202 us (0.89)
  waiting for transfers between devices: 103 us -> 75.5 us
  local copies, waits for them, and re-layouts: 8.8 us -> 5.9 us
    psum x1, waiting for transfers between devices: 43.6 us -> 22.2 us  [per_device(): dense_parts = lax.psum((dense_parts[0], dense_parts[1]), 'grp')]
    all_to_all x1, waiting for transfers between devices: 21.3 us -> 0.01 us  [per_device(): lax.all_to_all(send_grads, 'dev', split_axis=1, concat_axis=0, tiled=True)]
    reduce_scatter x1, waiting for transfers between devices: 30.2 us -> 47 us  [per_device(): lax.psum_scatter(weight_term, 'dev', scatter_dimension=0, tiled=True)]
    unnamed x19 -> x20, local copies, waits for them, and re-layouts: 4.8 us -> 1.9 us
    reduce_sum x0 -> x1, other arithmetic: none -> 2.88 us  [per_device(): table_grad = jnp.sum(parts, axis=0)]
  transfers between devices with their start and end apart: 6 -> 7, of which waited for: 5 -> 4; matrix products, arithmetic and copies ran while one was open for 8% -> 9% of each run, Pallas kernels for 0% -> 0%
where the time goes in v1:
time: 202 us; the launch traced here: 201 us
  waiting for transfers between devices  75.5 us (37%)
  blocking collectives  67.8 us (34%)
  starting transfers between devices  16.7 us (8%)
  between operations  15.4 us (8%)
  matrix products  10.6 us (5%)
  other arithmetic  9.41 us (5%)
  local copies, waits for them, and re-layouts  5.9 us (3%)
    unnamed x2, blocking collectives  62.9 us
    reduce_scatter x1, waiting for transfers between devices, per_device(): lax.psum_scatter(weight_term, 'dev', scatter_dimension=0, tiled=True)  47 us
    psum x1, waiting for transfers between devices, per_device(): dense_parts = lax.psum((dense_parts[0], dense_parts[1]), 'grp')  22.2 us
    dot_general x4, matrix products, add_block(): jnp.dot(counts.astype(jnp.bfloat16), values, preferred_element_type=jnp.f...  8.37 us
    all_to_all x1, starting transfers between devices, per_device(): lax.all_to_all(send_exps, 'dev', split_axis=1, concat_axis=0, tiled=True)  7.39 us
    all_to_all x1, waiting for transfers between devices, per_device(): lax.all_to_all(send_rows, 'dev', split_axis=1, concat_axis=0, tiled=True)  5.76 us
    all_to_all x1, starting transfers between devices, per_device(): lax.all_to_all(send_rows, 'dev', split_axis=1, concat_axis=0, tiled=True)  5.49 us
    psum x1, blocking collectives, per_device(): dense_parts = lax.psum((dense_parts[0], dense_parts[1]), 'grp')  4.93 us
  transfers between devices with their start and end apart: 7, of which 4 were waited for; matrix products, arithmetic and copies ran while one was open for 9% of the time, Pallas kernels for 0%

profile of v1, /device:TPU:0, one launch (start us, length us, event | category | flops | bytes accessed | tf_op | source)
XLA Modules:
  0.0 201.5 jit_solution(13847989534407465325)
XLA Ops:
  7.2 0.0 copy-start
  7.2 0.7 compare_select_fusion.5
  7.9 0.7 scatter_custom_fusion
  8.6 0.1 broadcast_in_dim.41
  8.7 1.3 gather_fusion.2
  10.0 0.7 broadcast_select_fusion.1
  10.7 7.4 %all-to-all-start.2 = ((s32[128,16,2]{0,2,1:T(2,128)}), s32[128,16,2]{0,2,1:T(2,128)S(1)}, u32[]{:S(2)}, u32[]{:S(2)}) async-start(s32[128,16,2]{0,2,1:T(2,128)} %broadcast_select_fusion.1), calls=%async_computation.2 | async-start | bytes 32768 | tf_op jit(solution)/shard_map/all_to_all | solution.py:76
  18.1 0.0 reduce-scatter.2.cloned.1.call-start
  18.2 2.3 %fusion.25 = f32[512,512]{1,0:T(8,128)} fusion(bf16[128,512]{1,0:T(8,128)(2,1)S(1)} %copy-done, bf16[128,512]{1,0:T(8,128)(2,1)} %param.15), kind=kOutput, calls=%fused_computation.62 | convolution fusion | flops 67108864 | bytes 1310720 | tf_op jit(solution)/shard_map/dot_general | solution.py:69
  20.4 0.0 reduce-scatter.2.cloned.1.call-update
  20.5 0.6 gather_fusion
  21.2 1.4 clamp_convert_fusion
  22.6 0.7 fusion.14
  23.3 0.7 gather_fusion.1
  24.1 0.5 all-to-all-done.2
  24.6 5.5 %all-to-all-start = ((s32[128,16,2,4]{0,2,3,1:T(2,128)}), s32[128,16,2,4]{0,2,3,1:T(2,128)S(1)}, u32[]{:S(2)}, u32[]{:S(2)}) async-start(s32[128,16,2,4]{0,2,3,1:T(2,128)} %fusion.14), calls=%async_computation | async-start | bytes 131072 | tf_op jit(solution)/shard_map/all_to_all | solution.py:75
  30.1 1.1 broadcast_select_fusion
  31.2 5.8 %all-to-all-done = s32[128,16,2,4]{0,2,3,1:T(2,128)S(1)} async-done(((s32[128,16,2,4]{0,2,3,1:T(2,128)}), s32[128,16,2,4]{0,2,3,1:T(2,128)S(1)}, u32[]{:S(2)}, u32[]{:S(2)}) %all-to-all-start) | async-done | bytes 65568 | tf_op jit(solution)/shard_map/all_to_all | solution.py:75
  37.0 3.7 %all-to-all-start.1 = ((bf16[128,16,2,128]{3,0,2,1:T(8,128)(2,1)}), bf16[128,16,2,128]{3,0,2,1:T(8,128)(2,1)S(1)}, u32[]{:S(2)}, u32[]{:S(2)}) async-start(bf16[128,16,2,128]{3,0,2,1:T(8,128)(2,1)} %broadcast_select_fusion), calls=%async_computation.1 | async-start | bytes 2097152 | tf_op jit(solution)/shard_map/all_to_all | solution.py:74
  40.7 0.0 all-reduce.4.cloned.1.call-start
  40.8 47.0 %reduce-scatter.2.cloned.1.call-done = f32[32,512]{1,0:T(8,128)} async-done(((f32[512,512]{1,0:T(8,128)}), f32[32,512]{1,0:T(8,128)}) %reduce-scatter.2.cloned.1.call-update) | async-done | bytes 65552 | tf_op jit(solution)/shard_map/reduce_scatter | solution.py:81
  87.8 0.0 all-reduce.4.cloned.1.call-update
  87.8 0.0 all-gather.4.cloned.1.call-start
  87.9 22.2 %all-reduce.4.cloned.1.call-done = f32[32,512]{1,0:T(8,128)} async-done(((f32[32,512]{1,0:T(8,128)}), f32[32,512]{1,0:T(8,128)}) %all-reduce.4.cloned.1.call-update) | async-done | bytes 65552 | tf_op jit(solution)/shard_map/psum | solution.py:84
  110.1 0.0 all-gather.4.cloned.1.call-update
  110.1 0.0 all-gather.6.cloned.1.call-start
  110.2 0.1 copy.26
  110.3 0.7 fusion.13
  111.0 4.5 %while.31 = (s32[]{:T(128)}, f32[1024,128]{1,0:T(8,128)S(1)}, s32[2048,4]{0,1:T(4,128)S(1)}, bf16[2048,128]{1,0:T(8,128)(2,1)S(1)}, s32[]{:T(128)}, /*index=5*/s...) while((s32[]{:T(128)}, f32[1024,128]{1,0:T(8,128)S(1)}, ...), condition=%wide.region_4.5_spmd.clone.clone, body=%wide.region_3.4_spmd.clone.clone.sunk | while | flops 281280512 | bytes 1360101 | solution.py:45
  111.0 0.1 constant_dynamic-slice_fusion.5
  111.2 2.1 %fusion.35 = f32[1024,128]{1,0:T(8,128)S(1)} fusion(s32[1024]{0:T(1024)S(1)} %bitcast.83, s32[1024]{0:T(1024)S(1)} %bitcast.81, s32[1024]{0:T(1024)S(1)} %bitcast.82, s32[1024]{0:T(1024)S(1)} %bitcast.80, f32[1024,128]{1,0:T(8,128)S(1)} %get-tuple-element.389, bf16[2048,128]{1,0:T(8,128)(2,1)S(1)} %get-tuple-element.402, s32[]{:T(128)S(6)} %select_n.64, ...), kind=kOutput, calls=%fused_computation.22.clone.1 | convolution fusion | flops 281280512 | bytes 1327109 | tf_op jit(solution)/shard_map/while/body/eval_jaxpr/dot_general | solution.py:40
  113.3 0.1 constant_dynamic-slice_fusion.5
  113.4 2.1 %fusion.35 = f32[1024,128]{1,0:T(8,128)S(1)} fusion(s32[1024]{0:T(1024)S(1)} %bitcast.83, s32[1024]{0:T(1024)S(1)} %bitcast.81, s32[1024]{0:T(1024)S(1)} %bitcast.82, s32[1024]{0:T(1024)S(1)} %bitcast.80, f32[1024,128]{1,0:T(8,128)S(1)} %get-tuple-element.389, bf16[2048,128]{1,0:T(8,128)(2,1)S(1)} %get-tuple-element.402, s32[]{:T(128)S(6)} %select_n.64, ...), kind=kOutput, calls=%fused_computation.22.clone.1 | convolution fusion | flops 281280512 | bytes 1327109 | tf_op jit(solution)/shard_map/while/body/eval_jaxpr/dot_general | solution.py:40
  115.5 4.5 %while.30 = (s32[]{:T(128)}, f32[1024,128]{1,0:T(8,128)S(1)}, s32[2048,4]{0,1:T(4,128)S(1)}, bf16[2048,128]{1,0:T(8,128)(2,1)S(1)}, s32[]{:T(128)}, /*index=5*/s...) while((s32[]{:T(128)}, f32[1024,128]{1,0:T(8,128)S(1)}, ...), condition=%wide.region_2.3_spmd.clone.clone, body=%wide.region_1.2_spmd.clone.clone.sunk | while | flops 281280512 | bytes 1360101 | solution.py:45
  115.5 0.1 constant_dynamic-slice_fusion.4
  115.6 2.1 %fusion.33 = f32[1024,128]{1,0:T(8,128)S(1)} fusion(s32[1024]{0:T(1024)S(1)} %bitcast.87, s32[1024]{0:T(1024)S(1)} %bitcast.85, s32[1024]{0:T(1024)S(1)} %bitcast.86, s32[1024]{0:T(1024)S(1)} %bitcast.84, f32[1024,128]{1,0:T(8,128)S(1)} %get-tuple-element.422, bf16[2048,128]{1,0:T(8,128)(2,1)S(1)} %get-tuple-element.435, s32[]{:T(128)S(6)} %select_n.63, ...), kind=kOutput, calls=%fused_computation.12.clone.1 | convolution fusion | flops 281280512 | bytes 1327109 | tf_op jit(solution)/shard_map/while/body/eval_jaxpr/dot_general | solution.py:40
  117.7 0.1 constant_dynamic-slice_fusion.4
  117.9 2.1 %fusion.33 = f32[1024,128]{1,0:T(8,128)S(1)} fusion(s32[1024]{0:T(1024)S(1)} %bitcast.87, s32[1024]{0:T(1024)S(1)} %bitcast.85, s32[1024]{0:T(1024)S(1)} %bitcast.86, s32[1024]{0:T(1024)S(1)} %bitcast.84, f32[1024,128]{1,0:T(8,128)S(1)} %get-tuple-element.422, bf16[2048,128]{1,0:T(8,128)(2,1)S(1)} %get-tuple-element.435, s32[]{:T(128)S(6)} %select_n.63, ...), kind=kOutput, calls=%fused_computation.12.clone.1 | convolution fusion | flops 281280512 | bytes 1327109 | tf_op jit(solution)/shard_map/while/body/eval_jaxpr/dot_general | solution.py:40
  120.0 1.0 pad_maximum_fusion
  121.0 0.0 all-gather.6.cloned.1.call-update
  121.1 0.6 fusion.24
  122.4 32.8 %all-reduce.1 = f32[512]{0:T(512)S(1)} all-reduce(f32[512]{0:T(512)S(1)} %convert_reduce_fusion), channel_id=4, replica_groups=mesh['grp'=2,'dev'=16] {'dev'}, use_global_device_ids=true, to_apply=%region_9.10.clone | all-reduce | flops 512 | bytes 4096
  155.2 0.1 dynamic-slice.2
  155.9 4.9 %psum.15 = f32[32]{0:T(128)S(1)} all-reduce(f32[32]{0:T(128)S(1)} %dynamic-slice.2), channel_id=1, replica_groups=mesh['grp'=2,'dev'=16] {'grp'}, use_global_device_ids=true, to_apply=%region_10.11 | all-reduce | flops 32 | bytes 256 | tf_op jit(solution)/shard_map/psum | solution.py:84
  160.9 0.2 dynamic-update-slice
  161.0 30.0 %all-reduce = f32[512]{0:T(512)} all-reduce(f32[512]{0:T(512)S(1)} %dynamic-update-slice), channel_id=1, replica_groups=mesh['grp'=2,'dev'=16] {'dev'}, use_global_device_ids=true, to_apply=%add | all-reduce | flops 512 | bytes 4096
  191.1 2.9 %reduce_sum.18 = f32[2,1024,128]{2,1,0:T(8,128)} reduce(f32[2,2,1024,128]{3,2,1,0:T(8,128)} %bitcast.74, f32[]{:T(128)} %constant.118.clone.1), dimensions={0}, to_apply=%region_5.6 | reduce | flops 262144 | bytes 3145732 | tf_op jit(solution)/shard_map/reduce_sum | solution.py:79
  194.0 1.0 copy.51
  (30 shorter events, 0.2 us)
Async XLA Ops:
  7.2 11.0 %copy-start = (bf16[128,512]{1,0:T(8,128)(2,1)S(1)}, bf16[128,512]{1,0:T(8,128)(2,1)}, u32[]{:S(2)}) copy-start(bf16[128,512]{1,0:T(8,128)(2,1)} %param.14) | copy-start | bytes 393220
  7.2 13.3 %copy-start.2 = (s32[128,32]{0,1:T(8,128)S(1)}, s32[128,32]{0,1:T(8,128)}, u32[]{:S(2)}) copy-start(s32[128,32]{0,1:T(8,128)} %param.12) | copy-start | bytes 49156
  7.2 13.3 %copy-start.1 = (s32[128,4,32]{0,2,1:T(8,128)S(1)}, s32[128,4,32]{0,2,1:T(8,128)}, u32[]{:S(2)}) copy-start(s32[128,4,32]{0,2,1:T(8,128)} %param.11) | copy-start | bytes 196612
  10.7 13.9 %all-to-all-start.2 = ((s32[128,16,2]{0,2,1:T(2,128)}), s32[128,16,2]{0,2,1:T(2,128)S(1)}, u32[]{:S(2)}, u32[]{:S(2)}) async-start(s32[128,16,2]{0,2,1:T(2,128)} %broadcast_select_fusion.1), calls=%async_computation.2 | async-start | bytes 32768 | tf_op jit(solution)/shard_map/all_to_all | solution.py:76
  18.1 3.1 %copy-start.3 = (bf16[128,32,128]{2,1,0:T(8,128)(2,1)S(1)}, bf16[128,32,128]{2,1,0:T(8,128)(2,1)}, u32[]{:S(2)}) copy-start(bf16[128,32,128]{2,1,0:T(8,128)(2,1)} %param.10) | copy-start | bytes 3145732
  18.1 69.7 %reduce-scatter.2.cloned.1.call-start = ((), (), s32[]{:S(2)}) async-start(), calls=%async_computation.4 | async-start | bytes 1114112 | tf_op jit(solution)/shard_map/reduce_scatter | solution.py:81
  24.6 12.4 %all-to-all-start = ((s32[128,16,2,4]{0,2,3,1:T(2,128)}), s32[128,16,2,4]{0,2,3,1:T(2,128)S(1)}, u32[]{:S(2)}, u32[]{:S(2)}) async-start(s32[128,16,2,4]{0,2,3,1:T(2,128)} %fusion.14), calls=%async_computation | async-start | bytes 131072 | tf_op jit(solution)/shard_map/all_to_all | solution.py:75
  37.0 73.2 %all-to-all-start.1 = ((bf16[128,16,2,128]{3,0,2,1:T(8,128)(2,1)}), bf16[128,16,2,128]{3,0,2,1:T(8,128)(2,1)S(1)}, u32[]{:S(2)}, u32[]{:S(2)}) async-start(bf16[128,16,2,128]{3,0,2,1:T(8,128)(2,1)} %broadcast_select_fusion), calls=%async_computation.1 | async-start | bytes 2097152 | tf_op jit(solution)/shard_map/all_to_all | solution.py:74
  40.7 69.4 %all-reduce.4.cloned.1.call-start = ((), (), s32[]{:S(2)}) async-start(), calls=%async_computation.5 | async-start | bytes 131072 | tf_op jit(solution)/shard_map/psum | solution.py:84
  87.8 103.3 %all-gather.4.cloned.1.call-start = ((), (), s32[]{:S(2)}) async-start(), calls=%async_computation.6 | async-start | bytes 1114112 | tf_op jit(solution)/shard_map/all_gather | solution.py:86
  110.1 81.0 %all-gather.6.cloned.1.call-start = ((), (), s32[]{:S(2)}) async-start(), calls=%async_computation.7 | async-start | bytes 3145728 | tf_op jit(solution)/shard_map/all_gather | solution.py:78
  120.0 1.1 copy-start.6
  120.0 2.3 %copy-start.5 = (bf16[128,512]{1,0:T(8,128)(2,1)S(1)}, bf16[128,512]{1,0:T(8,128)(2,1)}, u32[]{:S(2)}) copy-start(bf16[128,512]{1,0:T(8,128)(2,1)} %param.15) | copy-start | bytes 393220
  191.1 2.9 %copy-start.4 = (f32[512,512]{1,0:T(8,128)S(1)}, f32[512,512]{1,0:T(8,128)}, u32[]{:S(2)}) copy-start(f32[512,512]{1,0:T(8,128)} %all-gather.4.cloned.1.call-done) | copy-start | bytes 3145732
Sparse Core Ops, SparseCore 0:
  23.1 64.6 reduce-scatter.1
  90.0 20.0 all-reduce.3
  112.3 37.8 all-gather.3
  152.2 31.9 all-gather.5
